TPU v7x, 256 devices: a whole 4x4x8 slice. The times are simulated.
256 devices in a mesh: row: 8 (over z), col: 32 (over x, y, core).
Axes of the slice: x: 4, y: 4, z: 8, core: 2. Of those that a mesh axis runs over, the one named last changes fastest.
Arguments:
- gradient: bfloat16 [28672, 8192], P('row', 'col'), may hold values from -6 to 6
- projector: bfloat16 [8192, 1024], P('col', 'row'), may hold values from -0.0625 to 0.0625
- first_moment: float32 [1024, 28672], P('col', 'row'), may hold values from -2 to 2
- second_moment: float32 [1024, 28672], P('col', 'row'), may hold values from 0.0001 to 0.01
Outputs:
- update: float32 [28672, 8192], P('row', 'col')
- first_next: float32 [1024, 28672], P('col', 'row')
- second_next: float32 [1024, 28672], P('col', 'row')
All inputs are finite; a program needn't handle non-finite values.
Results may differ from a plain program's by a relative error of at most 0.0058.
Values may be sent and summed in bfloat16 or wider, within the bound.
No kernel may reach another device: no remote copies, remote signals or barrier semaphores. Data moves between devices by JAX's collectives and lax.ppermute only.
A program may use at most 64 MiB of HBM per device.

v0:
```python
import jax
import jax.numpy as jnp
from jax import lax
from jax.sharding import PartitionSpec as P


def in_order(pieces, dim):
    lengths = list(pieces.shape[1:])
    lengths[dim] *= pieces.shape[0]
    return jnp.moveaxis(pieces, 0, dim).reshape(lengths)


def sent_to_all(x, axis):
    peers = lax.axis_size(axis)
    return lax.all_to_all(jnp.broadcast_to(x[None], (peers, *x.shape)), axis, 0, 0, tiled=True)


def gathered_copies(x, axis, dim):
    return in_order(sent_to_all(x, axis), dim)


def in_blocks(x, dim, peers):
    before, after = (x.shape[:dim], x.shape[dim + 1 :])
    return jnp.moveaxis(x.reshape(*before, peers, -1, *after), dim, 0)


def sum_at_owner(x, axis, dim):
    peers = lax.axis_size(axis)
    pieces = lax.all_to_all(in_blocks(x, dim, peers), axis, 0, 0, tiled=True)
    return jnp.sum(pieces.astype(jnp.float32), axis=0)


def adam_moments(compressed, first_moment, second_moment):
    first_next = 0.9 * first_moment + 0.1 * compressed
    second_next = 0.999 * second_moment + 0.001 * compressed * compressed
    corr_first = 1.0 - 0.9**10
    corr_second = 1.0 - 0.999**10
    direction = (first_next / corr_first / (jnp.sqrt(second_next / corr_second) + 1e-08)).astype(
        jnp.bfloat16
    )
    return (direction, first_next, second_next)


def shards(gradient, projector, first_moment, second_moment):
    proj_rows = gathered_copies(projector, "row", 1)
    proj_part = proj_rows
    compressed = sum_at_owner(
        lax.dot_general(
            proj_part, gradient, (((0,), (1,)), ((), ())), preferred_element_type=jnp.float32
        ).astype(jnp.bfloat16),
        "col",
        0,
    )
    direction, first_next, second_next = adam_moments(compressed, first_moment, second_moment)
    proj_part = proj_rows
    update = lax.dot_general(
        lax.all_gather(direction, "col", axis=0, tiled=True),
        proj_part,
        (((0,), (1,)), ((), ())),
        preferred_element_type=jnp.float32,
    )
    return (update, first_next, second_next)


def solution(mesh):
    return jax.shard_map(
        shards,
        mesh=mesh,
        in_specs=(P("row", "col"), P("col", "row"), P("col", "row"), P("col", "row")),
        out_specs=(P("row", "col"), P("col", "row"), P("col", "row")),
        check_vma=False,
    )
```

profile of v0, /device:TPU:1, one launch (start us, length us, event | category | flops | bytes accessed | tf_op | source)
XLA Modules:
  0.0 193.9 jit_solution(3954843862253366872)
XLA Ops:
  7.2 0.0 copy-start
  7.2 0.0 all-gather.2.cloned.1.call-start
  7.2 1.1 copy.7
  8.3 24.9 %all_to_all.10 = bf16[8,256,128]{1,2,0:T(8,128)(2,1)S(1)} all-to-all(bf16[8,256,128]{1,2,0:T(8,128)(2,1)S(1)} %broadcast_in_dim.2), channel_id=1, replica_groups=mesh['row'=8,'col'=32] {'row'}, dimensions={0} | all-to-all | bytes 1048576 | tf_op jit(solution)/shard_map/all_to_all | solution.py:15
  33.3 0.0 copy-done
  33.3 2.1 %convolution_convert_fusion = bf16[1024,3584]{1,0:T(8,128)(2,1)S(1)} fusion(bf16[256,1024]{0,1:T(8,128)(2,1)S(1)} %bitcast.9, bf16[3584,256]{1,0:T(8,128)(2,1)S(1)} %copy-done), kind=kOutput, calls=%fused_computation.1 | convolution fusion | flops 1882718208 | bytes 9699328 | tf_op jit(solution)/shard_map/dot_general | solution.py:48
  35.4 93.5 %all_to_all.11 = bf16[32,32,3584]{2,1,0:T(8,128)(2,1)S(1)} all-to-all(bf16[32,32,3584]{2,1,0:T(8,128)(2,1)S(1)} %bitcast.8), channel_id=1, replica_groups=mesh['row'=8,'col'=32] {'col'}, dimensions={0} | all-to-all | bytes 14680064 | tf_op jit(solution)/shard_map/all_to_all | solution.py:29
  128.9 0.0 copy-start.1
  128.9 0.0 copy-start.2
  128.9 1.0 convert_reduce_fusion
  129.9 0.0 copy-done.1
  130.0 0.1 copy-done.2
  130.1 1.1 divide_convert_fusion
  131.2 0.0 all-gather.2.cloned.1.call-update
  131.2 48.8 %all-gather.2.cloned.1.call-done = bf16[1024,3584]{1,0:T(8,128)(2,1)} async-done(((bf16[32,3584]{1,0:T(8,128)(2,1)}), bf16[1024,3584]{1,0:T(8,128)(2,1)}) %all-gather.2.cloned.1.call-update) | async-done | bytes 7340048 | tf_op jit(solution)/shard_map/all_gather | solution.py:57
  180.1 7.0 %fusion.2 = f32[3584,256]{1,0:T(8,128)} fusion(bf16[1024,3584]{1,0:T(8,128)(2,1)} %all-gather.2.cloned.1.call-done, bf16[256,1024]{0,1:T(8,128)(2,1)S(1)} %bitcast.10), kind=kOutput, calls=%fused_computation.6 | convolution fusion | flops 1879048192 | bytes 11534336 | tf_op jit(solution)/shard_map/dot_general | solution.py:56
  (1 shorter events, 0.0 us)
Async XLA Ops:
  7.2 26.1 %copy-start = (bf16[3584,256]{1,0:T(8,128)(2,1)S(1)}, bf16[3584,256]{1,0:T(8,128)(2,1)}, u32[]{:S(2)}) copy-start(bf16[3584,256]{1,0:T(8,128)(2,1)} %param.4) | copy-start | bytes 5505028
  7.2 172.9 %all-gather.2.cloned.1.call-start = ((), (), s32[]{:S(2)}) async-start(), calls=%async_computation.2 | async-start | bytes 7569408 | tf_op jit(solution)/shard_map/all_gather | solution.py:57
  128.9 1.0 copy-start.1
  128.9 1.2 copy-start.2
Sparse Core Ops, SparseCore 0:
  131.4 48.6 all-gather.1
where the time goes:
time: 194 us
  blocking collectives  118 us (61%)
  waiting for transfers between devices  48.8 us (25%)
  between operations  14.1 us (7%)
  matrix products  9.14 us (5%)
  other arithmetic  2.17 us (1%)
    all_to_all x1, blocking collectives, sum_at_owner(): pieces = lax.all_to_all(in_blocks(x, dim, peers), axis, 0, 0, tiled=True)  93.5 us
    all_gather x1, waiting for transfers between devices, shards(): lax.all_gather(direction, 'col', axis=0, tiled=True)  48.8 us
    all_to_all x1, blocking collectives, sent_to_all(): lax.all_to_all(jnp.broadcast_to(x[None], (peers, *x.shape)), axis, 0, 0,...  24.9 us
    dot_general x1, matrix products, shards(): lax.dot_general(lax.all_gather(direction, 'col', axis=0, tiled=True), pro...  7.03 us
  transfers between devices with their start and end apart: 1, of which 1 were waited for; matrix products, arithmetic and copies ran while one was open for 0% of the time, Pallas kernels for 0%

commit v1 on v0

--- a/solution.py
+++ b/solution.py
@@ -2,6 +2,18 @@
 import jax.numpy as jnp
 from jax import lax
 from jax.sharding import PartitionSpec as P
+
+
+def doubled_up(x, axis, dim):
+    ways, here = (lax.axis_size(axis), lax.axis_index(axis))
+    grown, reach = (x, 1)
+    while reach < ways:
+        theirs = lax.ppermute(grown, axis, [(d, d ^ reach) for d in range(ways)])
+        mine_first = jnp.concatenate([grown, theirs], axis=dim)
+        theirs_first = jnp.concatenate([theirs, grown], axis=dim)
+        grown = jnp.where(here & reach == 0, mine_first, theirs_first)
+        reach = 2 * reach
+    return grown
 
 
 def in_order(pieces, dim):
@@ -54,7 +66,7 @@
     direction, first_next, second_next = adam_moments(compressed, first_moment, second_moment)
     proj_part = proj_rows
     update = lax.dot_general(
-        lax.all_gather(direction, "col", axis=0, tiled=True),
+        doubled_up(direction, "col", 0),
         proj_part,
         (((0,), (1,)), ((), ())),
         preferred_element_type=jnp.float32,

time: 194 us -> 300 us (1.55)
  waiting for transfers between devices: 48.8 us -> 153 us
  between operations: 14.1 us -> 0.71 us
  other arithmetic: 2.17 us -> 12.1 us
    ppermute x0 -> x5, waiting for transfers between devices: none -> 153 us  [doubled_up(): theirs = lax.ppermute(grown, axis, [(d, d ^ reach) for d in range(ways)])]
    all_gather x1 -> x0, waiting for transfers between devices: 48.8 us -> none  [shards(): lax.all_gather(direction, 'col', axis=0, tiled=True)]
    select_n x0 -> x4, other arithmetic: none -> 9.85 us  [doubled_up(): grown = jnp.where(here & reach == 0, mine_first, theirs_first)]
  transfers between devices with their start and end apart: 1 -> 5, of which waited for: 1 -> 5; matrix products, arithmetic and copies ran while one was open for 0% -> 0% of each run, Pallas kernels for 0% -> 0%
where the time goes in v1:
time: 300 us; the launch traced here: 299 us
  waiting for transfers between devices  153 us (51%)
  blocking collectives  118 us (39%)
  other arithmetic  12.1 us (4%)
  matrix products  9.92 us (3%)
    ppermute x5, waiting for transfers between devices, doubled_up(): theirs = lax.ppermute(grown, axis, [(d, d ^ reach) for d in range(ways)])  153 us
    all_to_all x1, blocking collectives, sum_at_owner(): pieces = lax.all_to_all(in_blocks(x, dim, peers), axis, 0, 0, tiled=True)  93.5 us
    all_to_all x1, blocking collectives, sent_to_all(): lax.all_to_all(jnp.broadcast_to(x[None], (peers, *x.shape)), axis, 0, 0,...  24.9 us
    select_n x4, other arithmetic, doubled_up(): grown = jnp.where(here & reach == 0, mine_first, theirs_first)  9.85 us
    dot_general x1, matrix products, shards(): lax.dot_general(doubled_up(direction, 'col', 0), proj_part, (((0,), (1,))...  7.81 us
  transfers between devices with their start and end apart: 5, of which 5 were waited for; matrix products, arithmetic and copies ran while one was open for 0% of the time, Pallas kernels for 0%

profile of v1, /device:TPU:1, one launch (start us, length us, event | category | flops | bytes accessed | tf_op | source)
XLA Modules:
  0.0 298.7 jit_solution(13951542499649732398)
XLA Ops:
  0.6 0.0 copy-start
  0.6 1.1 copy.7
  1.8 24.9 %all_to_all.10 = bf16[8,256,128]{1,2,0:T(8,128)(2,1)S(1)} all-to-all(bf16[8,256,128]{1,2,0:T(8,128)(2,1)S(1)} %broadcast_in_dim.2), channel_id=1, replica_groups=mesh['row'=8,'col'=32] {'row'}, dimensions={0} | all-to-all | bytes 1048576 | tf_op jit(solution)/shard_map/all_to_all | solution.py:27
  26.7 0.0 copy-done
  26.7 2.1 convolution_convert_fusion
  28.8 93.5 %all_to_all.11 = bf16[32,32,3584]{2,1,0:T(8,128)(2,1)S(1)} all-to-all(bf16[32,32,3584]{2,1,0:T(8,128)(2,1)S(1)} %bitcast.7), channel_id=1, replica_groups=mesh['row'=8,'col'=32] {'col'}, dimensions={0} | all-to-all | bytes 14680064 | tf_op jit(solution)/shard_map/all_to_all | solution.py:41
  122.3 0.0 copy-start.2
  122.3 0.0 copy-start.3
  122.3 1.0 convert_reduce_fusion
  123.4 0.0 copy-done.2
  123.4 0.1 copy-done.3
  123.5 1.2 divide_convert_fusion
  124.7 0.1 collective-permute-start
  124.8 1.4 collective-permute-done
  126.2 0.1 maximum_select_fusion.5
  126.3 0.0 copy-start.1
  126.3 0.1 collective-permute-start.1
  126.4 0.7 copy-done.1
  127.0 11.4 %collective-permute-done.1 = bf16[64,3584]{1,0:T(8,128)(2,1)} collective-permute-done((bf16[64,3584]{1,0:T(8,128)(2,1)S(1)}, bf16[64,3584]{1,0:T(8,128)(2,1)}, u32[]{:S(2)}, u32[]{:S(2)}) %collective-permute-start.1) | collective-permute-done | bytes 458784 | tf_op jit(solution)/shard_map/ppermute | solution.py:11
  138.4 1.6 maximum_select_fusion.4
  140.1 1.1 collective-permute-start.2
  141.2 21.5 %collective-permute-done.2 = bf16[128,3584]{1,0:T(8,128)(2,1)} collective-permute-done((bf16[128,3584]{1,0:T(8,128)(2,1)S(1)}, bf16[128,3584]{1,0:T(8,128)(2,1)}, u32[]{:S(2)}, u32[]{:S(2)}) %collective-permute-start.2) | collective-permute-done | bytes 917536 | tf_op jit(solution)/shard_map/ppermute | solution.py:11
  162.7 3.1 %maximum_select_fusion.3 = bf16[256,3584]{1,0:T(8,128)(2,1)} fusion(bf16[128,3584]{1,0:T(8,128)(2,1)} %collective-permute-done.2, bf16[128,3584]{1,0:T(8,128)(2,1)S(1)} %maximum_select_fusion.4, pred[]{:T(512)S(6)} %eq.17), kind=kLoop, calls=%fused_computation.11 | loop fusion | flops 8257536 | bytes 3670017 | tf_op jit(solution)/shard_map/jit(_where)/select_n | solution.py:14
  165.8 0.0 collective-permute-start.3
  165.8 40.0 %collective-permute-done.3 = bf16[256,3584]{1,0:T(8,128)(2,1)} collective-permute-done((bf16[256,3584]{1,0:T(8,128)(2,1)}, bf16[256,3584]{1,0:T(8,128)(2,1)}, u32[]{:S(2)}, u32[]{:S(2)}) %collective-permute-start.3) | collective-permute-done | bytes 1835040 | tf_op jit(solution)/shard_map/ppermute | solution.py:11
  205.9 5.0 %maximum_select_fusion.2 = bf16[512,3584]{1,0:T(8,128)(2,1)} fusion(bf16[256,3584]{1,0:T(8,128)(2,1)} %collective-permute-done.3, bf16[256,3584]{1,0:T(8,128)(2,1)} %maximum_select_fusion.3, pred[]{:T(512)S(6)} %eq.16), kind=kLoop, calls=%fused_computation.10 | loop fusion | flops 16515072 | bytes 7340033 | tf_op jit(solution)/shard_map/jit(_where)/select_n | solution.py:14
  210.8 1.2 collective-permute-start.4
  212.1 78.8 %collective-permute-done.4 = bf16[512,3584]{1,0:T(8,128)(2,1)} collective-permute-done((bf16[512,3584]{1,0:T(8,128)(2,1)}, bf16[512,3584]{1,0:T(8,128)(2,1)}, u32[]{:S(2)}, u32[]{:S(2)}) %collective-permute-start.4) | collective-permute-done | bytes 3670048 | tf_op jit(solution)/shard_map/ppermute | solution.py:11
  290.9 7.8 %fusion = f32[3584,256]{1,0:T(8,128)} fusion(bf16[256,1024]{0,1:T(8,128)(2,1)S(1)} %bitcast.9, bf16[512,3584]{1,0:T(8,128)(2,1)} %collective-permute-done.4, bf16[512,3584]{1,0:T(8,128)(2,1)} %maximum_select_fusion.2, pred[]{:T(512)S(6)} %eq.15), kind=kOutput, calls=%fused_computation.3 | convolution fusion | flops 1912078336 | bytes 11534337 | tf_op jit(solution)/shard_map/dot_general | solution.py:68
  (1 shorter events, 0.0 us)
Async XLA Ops:
  0.6 26.1 %copy-start = (bf16[3584,256]{1,0:T(8,128)(2,1)S(1)}, bf16[3584,256]{1,0:T(8,128)(2,1)}, u32[]{:S(2)}) copy-start(bf16[3584,256]{1,0:T(8,128)(2,1)} %param.4) | copy-start | bytes 5505028
  122.3 1.0 copy-start.2
  122.3 1.2 copy-start.3
  124.7 1.5 collective-permute-start
  126.3 0.8 copy-start.1
  126.3 12.1 %collective-permute-start.1 = (bf16[64,3584]{1,0:T(8,128)(2,1)S(1)}, bf16[64,3584]{1,0:T(8,128)(2,1)}, u32[]{:S(2)}, u32[]{:S(2)}) collective-permute-start(bf16[64,3584]{1,0:T(8,128)(2,1)S(1)} %maximum_select_fusion.5), channel_id=1, source_target_pairs={{0,2},{1,3},{2,0},{3,1},{4,6},{5,7},{6,4},{7,5},{8,10},{9,11},{10,... | collective-permute-start | bytes 1376264 | tf_op jit(solution)/shard_map/ppermute | solution.py:11
  140.1 22.6 %collective-permute-start.2 = (bf16[128,3584]{1,0:T(8,128)(2,1)S(1)}, bf16[128,3584]{1,0:T(8,128)(2,1)}, u32[]{:S(2)}, u32[]{:S(2)}) collective-permute-start(bf16[128,3584]{1,0:T(8,128)(2,1)S(1)} %maximum_select_fusion.4), channel_id=1, source_target_pairs={{0,4},{1,5},{2,6},{3,7},{4,0},{5,1},{6,2},{7,3},{8,12},{9,13},{10,... | collective-permute-start | bytes 2752520 | tf_op jit(solution)/shard_map/ppermute | solution.py:11
  165.8 40.0 %collective-permute-start.3 = (bf16[256,3584]{1,0:T(8,128)(2,1)}, bf16[256,3584]{1,0:T(8,128)(2,1)}, u32[]{:S(2)}, u32[]{:S(2)}) collective-permute-start(bf16[256,3584]{1,0:T(8,128)(2,1)} %maximum_select_fusion.3), channel_id=1, source_target_pairs={{0,8},{1,9},{2,10},{3,11},{4,12},{5,13},{6,14},{7,15},{8,0},{9,1},... | collective-permute-start | bytes 5505032 | tf_op jit(solution)/shard_map/ppermute | solution.py:11
  210.8 80.0 %collective-permute-start.4 = (bf16[512,3584]{1,0:T(8,128)(2,1)}, bf16[512,3584]{1,0:T(8,128)(2,1)}, u32[]{:S(2)}, u32[]{:S(2)}) collective-permute-start(bf16[512,3584]{1,0:T(8,128)(2,1)} %maximum_select_fusion.2), channel_id=1, source_target_pairs={{0,16},{1,17},{2,18},{3,19},{4,20},{5,21},{6,22},{7,23},{8,24},{9,... | collective-permute-start | bytes 11010056 | tf_op jit(solution)/shard_map/ppermute | solution.py:11
